TPU v7x, 32 devices: a whole 2x2x4 slice. The times are simulated.
32 devices in a mesh: group: 8 (over z, y), local: 4 (over x, core).
Axes of the slice: x: 2, y: 2, z: 4, core: 2. Of those that a mesh axis runs over, the one named last changes fastest.
Arguments:
- dense_vec: bfloat16 [4096, 128], P(('group', 'local')), may hold values from -6 to 6
- q_tables: float32 [1024, 26, 128], P('group'), may hold values from -4 to 4
- r_tables: float32 [256, 26, 128], P('local'), may hold values from -4 to 4
- owner: int32 [4096, 26, 1], P(('group', 'local')), may hold values from 0 to 7; in each aligned block of 3328 rows (0 to 3327, 3328 to 6655, ..., all dimensions but the last counted through in order) at most 832 rows name the same one
- q_local: int32 [4096, 26], P(('group', 'local')), may hold values from 0 to 127
- r_index: int32 [4096, 26], P(('group', 'local')), may hold values from 0 to 255
- w_one: bfloat16 [479, 1024], replicated, may hold values from -0.25 to 0.25
- b_one: float32 [1024], replicated, may hold values from -3 to 3
- w_two: bfloat16 [1024, 1024], replicated, may hold values from -0.1875 to 0.1875
- b_two: float32 [1024], replicated, may hold values from -3 to 3
- w_three: bfloat16 [1024, 512], replicated, may hold values from -0.1875 to 0.1875
- b_three: float32 [512], replicated, may hold values from -3 to 3
- w_four: bfloat16 [512, 256], replicated, may hold values from -0.25 to 0.25
- b_four: float32 [256], replicated, may hold values from -3 to 3
- cotangent: bfloat16 [4096, 256], P(('group', 'local')), may hold values from -6 to 6
Outputs:
- q_new: float32 [1024, 26, 128], P('group')
- r_new: float32 [256, 26, 128], P('local')
- w_one_new: float32 [479, 1024], replicated
- b_one_new: float32 [1024], replicated
- w_two_new: float32 [1024, 1024], replicated
- b_two_new: float32 [1024], replicated
- w_three_new: float32 [1024, 512], replicated
- b_three_new: float32 [512], replicated
- w_four_new: float32 [512, 256], replicated
- b_four_new: float32 [256], replicated
Inputs may be any that keep to these rules, and one draw needn't show every extreme that they name: `owner`: within the rows of one device (its 128 samples times 26 tables), no group is named more than 832 times, a bound that some block reaches.
All inputs are finite; a program needn't handle non-finite values.
Results may differ from a plain program's by a relative error of at most 0.0025.
Values may be sent and summed in bfloat16 or wider, within the bound.
A program may use at most 128 MiB of HBM per device.

v0:
```python
import jax
import jax.numpy as jnp
import numpy as np
from jax import lax
from jax.sharding import PartitionSpec as P

table_rate = 0.05
dense_rate = 0.0005


def silu_slope(preact):
    sigma = jax.nn.sigmoid(preact)
    return sigma * (1.0 + preact * (1.0 - sigma))


def interact(dense_rows, embeds):
    vectors_all = jnp.concatenate([dense_rows[:, None, :], embeds], axis=1).astype(jnp.float32)
    gram_mat = jnp.einsum("bid,bjd->bij", vectors_all, vectors_all, precision=lax.Precision.HIGHEST)
    lower_i, lower_j = np.tril_indices(vectors_all.shape[1], -1)
    pair_vals = gram_mat[:, lower_i, lower_j]
    features = jnp.concatenate([dense_rows.astype(jnp.float32), pair_vals], axis=1).astype(
        jnp.bfloat16
    )
    return (vectors_all, features)


def pair_back(d_pairs, vectors_all):
    vectors = vectors_all.shape[1]
    lower_i, lower_j = np.tril_indices(vectors, -1)
    spread = (
        jnp.zeros((vectors_all.shape[0], vectors, vectors), jnp.float32)
        .at[:, lower_i, lower_j]
        .set(d_pairs)
    )
    spread = spread + jnp.swapaxes(spread, 1, 2)
    return jnp.einsum("bij,bjd->bid", spread, vectors_all, precision=lax.Precision.HIGHEST)


def contract_rows(left, right):
    return lax.dot_general(
        left, right, (((0,), (0,)), ((), ())), preferred_element_type=jnp.float32
    )


def dense_pass(features, layers, cot_rows):
    inputs_list = [features]
    pre_list = []
    current = features
    for layer_idx, (weight, biases) in enumerate(layers):
        pre_act = jnp.dot(current, weight, preferred_element_type=jnp.float32) + biases
        pre_list.append(pre_act)
        if layer_idx + 1 < len(layers):
            current = jax.nn.silu(pre_act).astype(jnp.bfloat16)
            inputs_list.append(current)
    grad_low = cot_rows
    grad_full = cot_rows.astype(jnp.float32)
    grads = []
    back_grad = None
    for layer_idx in reversed(range(len(layers))):
        weight = layers[layer_idx][0]
        w_grad = contract_rows(inputs_list[layer_idx], grad_low)
        b_grad = jnp.sum(grad_full, axis=0)
        back_grad = lax.dot_general(
            grad_low, weight, (((1,), (1,)), ((), ())), preferred_element_type=jnp.float32
        )
        grads.insert(0, (w_grad, b_grad))
        if layer_idx > 0:
            grad_full = back_grad * silu_slope(pre_list[layer_idx - 1])
            grad_low = grad_full.astype(jnp.bfloat16)
    return (grads, back_grad)


def body(
    dense_vec,
    q_tables,
    r_tables,
    owner,
    q_local,
    r_index,
    w_one,
    b_one,
    w_two,
    b_two,
    w_three,
    b_three,
    w_four,
    b_four,
    cotangent,
):
    layers = [(w_one, b_one), (w_two, b_two), (w_three, b_three), (w_four, b_four)]
    groups = lax.axis_size("group")
    batch_rows, table_count = q_local.shape
    embed_width = q_tables.shape[2]
    lookups = batch_rows * table_count
    capacity = 2 * lookups // groups
    slot_count = groups * capacity
    segment_count = q_tables.shape[0] * table_count
    table_ids = jnp.arange(table_count, dtype=jnp.int32)[None, :]
    highest = lax.Precision.HIGHEST
    dest_group = owner[:, :, 0]
    owner_hits = (
        dest_group[:, :, None] == jnp.arange(groups, dtype=jnp.int32)[None, None, :]
    ).astype(jnp.float32)
    table_lower = (jnp.arange(table_count)[:, None] < jnp.arange(table_count)[None, :]).astype(
        jnp.float32
    )
    sample_lower = (jnp.arange(batch_rows)[:, None] < jnp.arange(batch_rows)[None, :]).astype(
        jnp.float32
    )
    within = jnp.einsum("st,bsg->btg", table_lower, owner_hits, precision=highest)
    before = jnp.einsum("cb,cg->bg", sample_lower, jnp.sum(owner_hits, axis=1), precision=highest)
    slot_rank = jnp.sum((within + before[:, None, :]) * owner_hits, axis=2).astype(jnp.int32)
    position = (dest_group * capacity + slot_rank).reshape(lookups)
    source = (
        jnp.full((slot_count,), lookups, jnp.int32)
        .at[position]
        .set(jnp.arange(lookups, dtype=jnp.int32))
    )
    row_keys = (q_local * table_count + table_ids).reshape(lookups)
    keys_padded = jnp.concatenate([row_keys, jnp.zeros((1,), jnp.int32)])
    outgoing = keys_padded[source].reshape(groups, capacity)
    flat_table = q_tables.reshape(segment_count, embed_width)
    request = lax.all_to_all(outgoing, "group", split_axis=0, concat_axis=0, tiled=True)
    served_rows = flat_table[request].astype(jnp.bfloat16)
    arrived = lax.all_to_all(served_rows, "group", split_axis=0, concat_axis=0, tiled=True)
    q_rows = arrived.reshape(slot_count, embed_width)[position]
    full_r = lax.all_gather(r_tables, "local", axis=0, tiled=True)
    remainder_count = full_r.shape[0]
    r_pick = (
        r_index[:, :, None] == jnp.arange(remainder_count, dtype=jnp.int32)[None, None, :]
    ).astype(jnp.float32)
    r_rows = jnp.einsum("btr,rtd->btd", r_pick, full_r, precision=highest).reshape(
        lookups, embed_width
    )
    q_val = q_rows.astype(jnp.float32)
    embeds = (q_val * r_rows).astype(jnp.bfloat16).reshape(batch_rows, table_count, embed_width)
    vectors_all, features = interact(dense_vec, embeds)
    grads, d_features = dense_pass(features, layers, cotangent)
    d_embed = pair_back(d_features[:, embed_width:], vectors_all)[:, 1:, :].reshape(
        lookups, embed_width
    )
    grad_padded = jnp.concatenate(
        [d_embed * r_rows, jnp.zeros((1, embed_width), jnp.float32)], axis=0
    )
    outbound = grad_padded[source].reshape(groups, capacity, embed_width)
    returned = (
        lax.all_to_all(
            outbound.astype(jnp.bfloat16), "group", split_axis=0, concat_axis=0, tiled=True
        )
        .astype(outbound.dtype)
        .reshape(slot_count, embed_width)
    )
    served_flat = request.reshape(slot_count)
    q_part = jax.ops.segment_sum(returned, served_flat, num_segments=segment_count).reshape(
        q_tables.shape
    )
    q_piece = lax.psum_scatter(
        q_part.astype(jnp.bfloat16), "local", scatter_dimension=0, tiled=True
    ).astype(jnp.float32)
    quarter = q_piece.shape[0]
    own_rows = lax.dynamic_slice_in_dim(q_tables, lax.axis_index("local") * quarter, quarter, 0)
    q_new = lax.all_gather(own_rows - table_rate * q_piece, "local", axis=0, tiled=True)
    r_part = jnp.einsum(
        "btr,btd->rtd",
        r_pick,
        (d_embed * q_val).reshape(batch_rows, table_count, embed_width),
        precision=highest,
    )
    summed = lax.psum(r_part, ("group", "local"))
    r_grad = lax.dynamic_slice_in_dim(
        summed, lax.axis_index("local") * r_tables.shape[0], r_tables.shape[0], 0
    )
    r_new = r_tables - table_rate * r_grad
    grad_wa, grad_ba, grad_wb, grad_bb, grad_wc, grad_bc, grad_wd, grad_bd = lax.psum(
        (
            grads[0][0],
            grads[0][1],
            grads[1][0],
            grads[1][1],
            grads[2][0],
            grads[2][1],
            grads[3][0],
            grads[3][1],
        ),
        ("group", "local"),
    )
    summed_grads = [(grad_wa, grad_ba), (grad_wb, grad_bb), (grad_wc, grad_bc), (grad_wd, grad_bd)]
    updated = []
    for (weight, biases), (w_grad, b_grad) in zip(layers, summed_grads):
        updated.append(weight.astype(jnp.float32) - dense_rate * w_grad)
        updated.append(biases - dense_rate * b_grad)
    return (
        q_new,
        r_new,
        updated[0],
        updated[1],
        updated[2],
        updated[3],
        updated[4],
        updated[5],
        updated[6],
        updated[7],
    )


def solution(mesh):
    return jax.shard_map(
        body,
        mesh=mesh,
        in_specs=(
            P(("group", "local"), None),
            P("group", None, None),
            P("local", None, None),
            P(("group", "local"), None, None),
            P(("group", "local"), None),
            P(("group", "local"), None),
            P(),
            P(),
            P(),
            P(),
            P(),
            P(),
            P(),
            P(),
            P(("group", "local"), None),
        ),
        out_specs=(
            P("group", None, None),
            P("local", None, None),
            P(),
            P(),
            P(),
            P(),
            P(),
            P(),
            P(),
            P(),
        ),
        check_vma=False,
    )
```

profile of v0, /device:TPU:0, one launch (start us, length us, event | category | flops | bytes accessed | tf_op | source)
XLA Modules:
  0.0 589.5 jit_solution(14401636984354006459)
XLA Ops:
  11.3 12.8 %scatter_custom_fusion = s32[6656]{0:T(1024)S(1)} fusion(s32[3328]{0:T(1024)S(1)} %fusion.38, s32[3328]{0:T(1024)S(1)} %iota.29, s32[]{:T(128)} %constant.27.clone.1), kind=kCustom, calls=%fused_computation.84 | custom fusion | bytes 26628 | tf_op jit(solution)/shard_map/scatter | solution.py:117
  24.1 34.5 %gather_fusion = s32[6656]{0:T(1024)S(1)} fusion(s32[3329]{0:T(1024)S(1)} %pad_add_fusion, s32[7168]{0:T(1024)S(1)} %pad_clamp_fusion.1), kind=kCustom, calls=%fused_computation | custom fusion | bytes 79872 | tf_op jit(solution)/shard_map/gather | solution.py:121
  59.4 7.3 %all-to-all-start = ((s32[8,1,832]{2,1,0:T(1,128)}), s32[8,1,832]{2,1,0:T(1,128)S(1)}, u32[]{:S(2)}, u32[]{:S(2)}) async-start(s32[8,1,832]{2,1,0:T(1,128)} %all_to_all.14), calls=%async_computation | async-start | bytes 57344 | tf_op jit(solution)/shard_map/all_to_all | solution.py:123
  66.7 2.5 copy.64
  69.4 4.0 all-to-all-done
  73.5 14.3 %gather_fusion.1 = bf16[6656,128]{1,0:T(8,128)(2,1)} fusion(bf16[3328,128]{1,0:T(8,128)(2,1)S(1)} %reshape.127, s32[7168]{0:T(1024)S(1)} %pad_clamp_fusion), kind=kCustom, calls=%fused_computation.1 | custom fusion | bytes 3434496 | tf_op jit(solution)/shard_map/gather | solution.py:124
  87.8 3.8 all-to-all-start.1
  91.7 38.3 %all-to-all-done.1 = bf16[8,832,128]{2,1,0:T(8,128)(2,1)S(1)} async-done(((bf16[8,832,128]{2,1,0:T(8,128)(2,1)}), bf16[8,832,128]{2,1,0:T(8,128)(2,1)S(1)}, u32[]{:S(2)}, u32[]{:S(2)}) %all-to-all-start.1) | async-done | bytes 1703968 | tf_op jit(solution)/shard_map/all_to_all | solution.py:125
  130.0 6.5 %gather_fusion.2 = bf16[3328,128]{1,0:T(8,128)(2,1)S(1)} fusion(bf16[6656,128]{1,0:T(8,128)(2,1)S(1)} %bitcast.53, s32[4096]{0:T(1024)S(1)} %pad_clamp_fusion.2), kind=kCustom, calls=%fused_computation.2 | custom fusion | bytes 1717248 | tf_op jit(solution)/shard_map/gather | solution.py:126
  137.2 7.3 %fusion.5 = (bf16[128,26,128]{2,0,1:T(8,128)(2,1)S(1)}, f32[26,128,128]{2,1,0:T(8,128)}) fusion(f32[128,26,128]{2,1,0:T(8,128)S(1)} %reshape.131, f32[256,26,128]{2,0,1:T(8,128)} %all-gather.3.cloned.1.call-done, s32[128,26]{0,1:T(8,128)S(1)} %copy-done.28), kind=kOutput, calls=%fused_computation.19 | convolution fusion | flops 1310326784 | bytes 7681024 | tf_op jit(solution)/shard_map/btr,rtd->btd/dot_general | solution.py:132
  146.4 4.9 gather_fusion.3
  152.9 2.3 convolution_add_fusion.1
  160.7 19.0 %scatter_fusion = f32[128,27,27]{0,2,1:T(8,128)S(1)} fusion(f32[128,27,27]{0,2,1:T(8,128)S(1)} %broadcast_in_dim.21, s32[351]{0:T(512)S(1)} %copy-done, f32[351,128]{1,0:T(8,128)S(1)} %convolution_bitcast_fusion), kind=kCustom, calls=%fused_computation.6 | custom fusion | bytes 541944 | tf_op jit(solution)/shard_map/scatter | solution.py:33
  180.0 2.9 copy.87
  182.9 3.3 fusion.14
  190.2 15.5 %gather_fusion.4 = bf16[6656,128]{1,0:T(8,128)(2,1)} fusion(bf16[3329,128]{1,0:T(8,128)(2,1)S(1)} %concatenate.24, s32[7168]{0:T(1024)} %copy-done.22), kind=kCustom, calls=%fused_computation.4 | custom fusion | bytes 3434496 | tf_op jit(solution)/shard_map/gather | solution.py:145
  205.7 4.4 all-to-all-start.2
  210.3 39.2 %all-to-all-done.2 = bf16[8,832,128]{2,1,0:T(8,128)(2,1)} async-done(((bf16[8,832,128]{2,1,0:T(8,128)(2,1)}), bf16[8,832,128]{2,1,0:T(8,128)(2,1)}, u32[]{:S(2)}, u32[]{:S(2)}) %all-to-all-start.2) | async-done | bytes 1703968 | tf_op jit(solution)/shard_map/all_to_all | solution.py:147
  249.5 45.6 %scatter_custom_fusion.2 = f32[3328,128]{1,0:T(8,128)} fusion(s32[6656]{0:T(1024)S(1)} %reshape.188, bf16[6656,128]{1,0:T(8,128)(2,1)} %bitcast.13, f32[]{:T(128)} %constant.24.clone.1), kind=kCustom, calls=%fused_computation.9 | custom fusion | flops 1703936 | bytes 3407876 | tf_op jit(solution)/shard_map/scatter-add | solution.py:154
  297.9 2.1 fusion.20
  301.7 1.8 fusion.28
  303.5 2.8 fusion.24
  306.3 6.2 %fusion.4 = f32[256,26,128]{0,2,1:T(8,128)} fusion(s32[128,26]{0,1:T(8,128)S(1)} %copy-done.28, f32[128,26,128]{2,1,0:T(8,128)S(1)} %fusion.14, f32[128,26,128]{2,1,0:T(8,128)S(1)} %copy-done.2), kind=kOutput, calls=%fused_computation.16 | convolution fusion | flops 1309900800 | bytes 6829056 | tf_op jit(solution)/shard_map/btr,btd->rtd/dot_general | solution.py:163
  312.6 8.3 %reduce-scatter.2.cloned.1.call-done = bf16[32,26,128]{2,1,0:T(8,128)(2,1)} async-done(((bf16[128,26,128]{2,1,0:T(8,128)(2,1)}), bf16[32,26,128]{2,1,0:T(8,128)(2,1)}) %reduce-scatter.2.cloned.1.call-update) | async-done | bytes 213008 | tf_op jit(solution)/shard_map/reduce_scatter | solution.py:157
  323.8 40.8 %all-reduce.1 = (f32[1024]{0:T(1024)S(1)}, f32[1024]{0:T(1024)S(1)}, f32[512]{0:T(512)S(1)}, f32[256]{0:T(256)S(1)}) all-reduce(f32[1024]{0:T(1024)S(1)} %copy-done.34, f32[1024]{0:T(1024)S(1)} %copy-done.33, f32[512]{0:T(512)S(1)} %copy-done.37, f32[256]{0:T(256)S(1)} %convert_reduce_fusion), channel_id=1, replica_groups=mesh['group'=8,'local'=4] {'group','local'}, use_global_device_ids=true, to_apply=%region_9.10 | all-reduce | flops 2816 | bytes 22528 | tf_op jit(solution)/shard_map/psum | solution.py:174
  366.3 192.3 %all-reduce.5.cloned.1.call-done = (f32[256,26,128]{0,2,1:T(8,128)}, f32[479,1024]{1,0:T(8,128)}, f32[1024,1024]{1,0:T(8,128)}, f32[1024,512]{1,0:T(8,128)}, f32[512,256]{1,0:T(8,128)}) async-done(((f32[256,26,128]{0,2,1:T(8,128)}, f32[479,1024]{1,0:T(8,128)}, f32[1024,1024]{1,0:T(8,128)}, f32[1024,512]{1,0:T(8,128)}, f32[512,256]{1,0:T(8,128)}), (f32[256,26,128]{0,2,1:T(8,128)}, f32[479,1024]{1,0:T(8,128)}, ...) | async-done | bytes 12185616 | tf_op jit(solution)/shard_map/psum | solution.py:169
  558.6 2.0 multiply_subtract_fusion.3
  561.9 1.9 multiply_subtract_fusion.4
  563.8 3.4 multiply_subtract_fusion.2
  570.3 2.7 multiply_subtract_fusion
  573.0 7.2 %all-gather.5.cloned.1.call-done = f32[128,26,128]{2,0,1:T(8,128)} async-done(((f32[32,26,128]{2,0,1:T(8,128)}), f32[128,26,128]{2,0,1:T(8,128)}) %all-gather.5.cloned.1.call-update) | async-done | bytes 1703952 | tf_op jit(solution)/shard_map/all_gather | solution.py:162
  580.2 2.8 copy.112
  (145 shorter events, 32.8 us)
Async XLA Ops:
  7.2 129.6 %all-gather.3.cloned.1.call-start = ((), (), s32[]{:S(2)}) async-start(), calls=%async_computation.4 | async-start | bytes 4259840 | tf_op jit(solution)/shard_map/all_gather | solution.py:127
  24.1 34.6 %copy-start.22 = (s32[7168]{0:T(1024)}, s32[7168]{0:T(1024)S(1)}, u32[]{:S(2)}) copy-start(s32[7168]{0:T(1024)S(1)} %pad_clamp_fusion.1) | copy-start | bytes 86020
  59.4 14.0 %all-to-all-start = ((s32[8,1,832]{2,1,0:T(1,128)}), s32[8,1,832]{2,1,0:T(1,128)S(1)}, u32[]{:S(2)}, u32[]{:S(2)}) async-start(s32[8,1,832]{2,1,0:T(1,128)} %all_to_all.14), calls=%async_computation | async-start | bytes 57344 | tf_op jit(solution)/shard_map/all_to_all | solution.py:123
  69.1 18.6 %copy-start.3 = (f32[128,26,128]{2,1,0:T(8,128)}, f32[128,26,128]{2,1,0:T(8,128)S(1)}, u32[]{:S(2)}) copy-start(f32[128,26,128]{2,1,0:T(8,128)S(1)} %copy.64) | copy-start | bytes 5111812
  73.3 14.4 %copy-start.23 = (s32[8,1,832]{2,1,0:T(1,128)}, s32[8,1,832]{2,1,0:T(1,128)S(1)}, u32[]{:S(2)}) copy-start(s32[8,1,832]{2,1,0:T(1,128)S(1)} %all-to-all-done) | copy-start | bytes 79876
  87.8 3.8 copy-start.25
  87.8 42.2 %all-to-all-start.1 = ((bf16[8,832,128]{2,1,0:T(8,128)(2,1)}), bf16[8,832,128]{2,1,0:T(8,128)(2,1)S(1)}, u32[]{:S(2)}, u32[]{:S(2)}) async-start(bf16[8,832,128]{2,1,0:T(8,128)(2,1)} %bitcast.55), calls=%async_computation.1 | async-start | bytes 3407872 | tf_op jit(solution)/shard_map/all_to_all | solution.py:125
  136.7 7.8 %copy-start.1 = (f32[128,26,128]{2,1,0:T(8,128)}, f32[128,26,128]{2,1,0:T(8,128)S(1)}, u32[]{:S(2)}) copy-start(f32[128,26,128]{2,1,0:T(8,128)S(1)} %reshape.131) | copy-start | bytes 5111812
  144.6 6.7 %copy-start.31 = (f32[1024]{0:T(1024)S(1)}, f32[1024]{0:T(1024)}, u32[]{:S(2)}) copy-start(f32[1024]{0:T(1024)} %param.30) | copy-start | bytes 12292
  145.3 7.6 %copy-start.32 = (f32[1024]{0:T(1024)S(1)}, f32[1024]{0:T(1024)}, u32[]{:S(2)}) copy-start(f32[1024]{0:T(1024)} %param.32) | copy-start | bytes 12292
  152.8 5.4 copy-start.11
  152.8 2.3 copy-start.14
  157.1 3.1 copy-start.26
  160.3 19.4 %copy-start.20 = (bf16[128,1024]{1,0:T(8,128)(2,1)}, bf16[128,1024]{1,0:T(8,128)(2,1)S(1)}, u32[]{:S(2)}) copy-start(bf16[128,1024]{1,0:T(8,128)(2,1)S(1)} %get-tuple-element.52) | copy-start | bytes 786436
  182.9 3.3 copy-start.4
  205.7 4.5 copy-start.24
  205.7 43.8 %all-to-all-start.2 = ((bf16[8,832,128]{2,1,0:T(8,128)(2,1)}), bf16[8,832,128]{2,1,0:T(8,128)(2,1)}, u32[]{:S(2)}, u32[]{:S(2)}) async-start(bf16[8,832,128]{2,1,0:T(8,128)(2,1)} %bitcast.54), calls=%async_computation.2 | async-start | bytes 3407872 | tf_op jit(solution)/shard_map/all_to_all | solution.py:147
  210.1 110.7 %reduce-scatter.2.cloned.1.call-start = ((), (), s32[]{:S(2)}) async-start(), calls=%async_computation.5 | async-start | bytes 1310720 | tf_op jit(solution)/shard_map/reduce_scatter | solution.py:157
  297.8 3.9 copy-start.18
  297.8 3.9 copy-start.27
  297.9 260.7 %all-reduce.5.cloned.1.call-start = ((), (), s32[]{:S(2)}) async-start(), calls=%async_computation.7 | async-start | bytes 24379392 | tf_op jit(solution)/shard_map/psum | solution.py:169
  300.0 3.5 copy-start.12
  303.5 2.8 copy-start.2
  312.5 10.7 %copy-start.8 = (f32[64,26,128]{2,0,1:T(8,128)S(1)}, f32[64,26,128]{2,0,1:T(8,128)}, u32[]{:S(2)}) copy-start(f32[64,26,128]{2,0,1:T(8,128)} %param.25) | copy-start | bytes 2555908
  312.5 267.7 %all-gather.5.cloned.1.call-start = ((), (), s32[]{:S(2)}) async-start(), calls=%async_computation.6 | async-start | bytes 2129920 | tf_op jit(solution)/shard_map/all_gather | solution.py:162
  322.1 42.4 %copy-start.38 = (f32[256]{0:T(256)S(1)}, f32[256]{0:T(256)}, u32[]{:S(2)}) copy-start(f32[256]{0:T(256)} %param.36) | copy-start | bytes 3076
  322.1 43.0 %copy-start.36 = (f32[512]{0:T(512)S(1)}, f32[512]{0:T(512)}, u32[]{:S(2)}) copy-start(f32[512]{0:T(512)} %param.34) | copy-start | bytes 6148
  560.5 3.3 copy-start.7
  561.9 5.3 copy-start.15
  563.8 3.4 copy-start.13
  563.8 5.1 copy-start.10
  567.3 3.0 copy-start.5
  (15 other events, 24.0 us)
Sparse Core Ops, SparseCore 0:
  9.5 32.7 all-gather.2
  298.0 22.8 reduce-scatter.1
  327.9 230.6 all-reduce.4
  560.5 19.5 all-gather.4
where the time goes:
time: 591 us; the launch traced here: 590 us
  waiting for transfers between devices  290 us (49%)
  local copies, waits for them, and re-layouts  130 us (22%)
  other arithmetic  64.9 us (11%)
  blocking collectives  40.8 us (7%)
  matrix products  34 us (6%)
  starting transfers between devices  15.7 us (3%)
  between operations  14.4 us (2%)
    psum x1, waiting for transfers between devices, body(): summed = lax.psum(r_part, ('group', 'local'))  192 us
    scatter-add x1, other arithmetic, body(): jax.ops.segment_sum(returned, served_flat, num_segments=segment_count)  45.6 us
    psum x1, blocking collectives, body(): lax.psum((grads[0][0], grads[0][1], grads[1][0], grads[1][1], grads[2][0]...  40.8 us
    all_to_all x1, waiting for transfers between devices, body(): lax.all_to_all(outbound.astype(jnp.bfloat16), 'group', split_axis=0, conc...  39.2 us
    all_to_all x1, waiting for transfers between devices, body(): lax.all_to_all(served_rows, 'group', split_axis=0, concat_axis=0, tiled=T...  38.3 us
    gather x1, local copies, waits for them, and re-layouts, body(): outgoing = keys_padded[source].reshape(groups, capacity)  34.5 us
    scatter x1, local copies, waits for them, and re-layouts, pair_back(): spread = jnp.zeros((vectors_all.shape[0], vectors, vectors), jnp.float32)...  19 us
    gather x1, local copies, waits for them, and re-layouts, body(): outbound = grad_padded[source].reshape(groups, capacity, embed_width)  15.5 us
  transfers between devices with their start and end apart: 7, of which 6 were waited for; matrix products, arithmetic and copies ran while one was open for 18% of the time, Pallas kernels for 0%

commit v1 on v0

v1 whole, which is shorter than its diff:
```python
import functools

import jax
import jax.numpy as jnp
from jax import lax
from jax.experimental import pallas as pl
from jax.experimental.pallas import tpu as pltpu
from jax.sharding import PartitionSpec as P

table_rate = 0.05
dense_rate = 0.0005
F32 = jnp.float32
BF16 = jnp.bfloat16
HIGHEST = lax.Precision.HIGHEST


def silu_slope(preact):
    sigma = jax.nn.sigmoid(preact)
    return sigma * (1.0 + preact * (1.0 - sigma))


def contract_rows(left, right):
    return lax.dot_general(left, right, (((0,), (0,)), ((), ())), preferred_element_type=F32)


def index_row(pack_ref, row):
    return jnp.concatenate(
        [pack_ref[s, 0, pl.ds(row, 1), :] for s in range(pack_ref.shape[0])], axis=1
    )


def pick_matrix(index, count):
    rows = lax.broadcasted_iota(jnp.int32, (count, index.shape[1]), 0)
    return rows == index.astype(jnp.int32)


def lookup_kernel(q_ref, pack_ref, emb_ref, q_out, r_out):
    groups, _, q_rows, width = q_ref.shape
    locals_, _, pack_rows, batch = pack_ref.shape
    r_rows = pack_rows - 8
    q_table = q_ref[:, 0].reshape(groups * q_rows, width)
    r_table = pack_ref[:, 0, :r_rows, :].reshape(locals_ * r_rows, width)
    q_hit = pick_matrix(index_row(pack_ref, r_rows), groups * q_rows).astype(F32).astype(BF16)
    r_hit = pick_matrix(index_row(pack_ref, r_rows + 1), locals_ * r_rows).astype(F32)
    over_rows = (((0,), (0,)), ((), ()))
    q_val = lax.dot_general(q_table, q_hit, over_rows, preferred_element_type=F32)
    r_val = lax.dot_general(
        r_table, r_hit, over_rows, preferred_element_type=F32, precision=HIGHEST
    )
    q_out[0] = q_val.astype(BF16)
    r_out[0] = r_val
    embeds = (q_val * r_val).astype(BF16)
    for s in range(locals_):
        emb_ref[s, 0] = embeds[:, s * batch : (s + 1) * batch]


def table_grad_kernel(d_ref, pack_ref, q_ref, r_ref, qg_ref, rg_ref):
    locals_, _, pack_rows, batch = pack_ref.shape
    r_rows = pack_rows - 8
    groups, _, q_rows, width = qg_ref.shape
    d_embed = jnp.concatenate([d_ref[s, 0] for s in range(locals_)], axis=1).astype(F32)
    q_hit = pick_matrix(index_row(pack_ref, r_rows), groups * q_rows).astype(F32).astype(BF16)
    r_hit = pick_matrix(index_row(pack_ref, r_rows + 1), locals_ * r_rows).astype(F32)
    over_lanes = (((1,), (1,)), ((), ()))
    q_terms = (d_embed * r_ref[0]).astype(BF16)
    r_terms = d_embed * q_ref[0].astype(F32)
    q_grad = lax.dot_general(q_hit, q_terms, over_lanes, preferred_element_type=F32)
    r_grad = lax.dot_general(
        r_hit, r_terms, over_lanes, preferred_element_type=F32, precision=HIGHEST
    )
    qg_ref[:, 0] = q_grad.astype(BF16).reshape(groups, q_rows, width)
    rg_ref[:, 0] = r_grad.reshape(locals_, r_rows, width)


def load_vectors(dense_ref, emb_ref, vec_ref, tables):
    vec_ref[0] = dense_ref[...].astype(F32)

    def fill(t, carry):
        vec_ref[t + 1] = emb_ref[t].astype(F32)
        return carry

    lax.fori_loop(0, tables, fill, 0)
    for t in range(tables + 1, vec_ref.shape[0]):
        vec_ref[t] = jnp.zeros(vec_ref.shape[1:], F32)


def gram_kernel(tables, dense_ref, emb_ref, feat_ref, vec_ref, row_ref):
    width = dense_ref.shape[0]
    load_vectors(dense_ref, emb_ref, vec_ref, tables)

    def outer(i, carry):
        mine = vec_ref[i]
        base = (i * (i - 1)) >> 1

        def inner(k, inner_carry):
            for u in range(4):
                j = 4 * k + u
                row_ref[pl.ds(base + j, 1), :] = jnp.sum(mine * vec_ref[j], axis=0, keepdims=True)
            return inner_carry

        return lax.fori_loop(0, (i + 3) >> 2, inner, carry)

    lax.fori_loop(1, tables + 1, outer, 0)
    pairs = feat_ref.shape[0] - width
    feat_ref[:width, :] = dense_ref[...]
    feat_ref[width:, :] = row_ref[:pairs, :].astype(BF16)


def pair_kernel(tables, d_ref, dense_ref, emb_ref, out_ref, vec_ref):
    width = dense_ref.shape[0]
    pairs = d_ref.shape[0] - width
    load_vectors(dense_ref, emb_ref, vec_ref, tables)

    def outer(i, carry):
        total = jnp.zeros(vec_ref.shape[1:], F32)
        for j in range(tables + 1):
            below = ((i * (i - 1)) >> 1) + j
            above = (j * (j - 1)) // 2 + i
            place = jnp.minimum(jnp.where(j < i, below, above), pairs - 1)
            row = d_ref[pl.ds(width + place, 1), :]
            row = jnp.where(i == j, jnp.zeros_like(row), row)
            total = total + row * vec_ref[j]
        out_ref[i - 1] = total.astype(BF16)
        return carry

    lax.fori_loop(1, tables + 1, outer, 0)
    for t in range(tables, out_ref.shape[0]):
        out_ref[t] = jnp.zeros(out_ref.shape[1:], BF16)


def whole(count):
    return [pl.BlockSpec(memory_space=pltpu.VMEM)] * count


def body(
    dense_vec,
    q_tables,
    r_tables,
    owner,
    q_local,
    r_index,
    w_one,
    b_one,
    w_two,
    b_two,
    w_three,
    b_three,
    w_four,
    b_four,
    cotangent,
):
    weights = [w_one, w_two, w_three, w_four]
    biases = [b_one, b_two, b_three, b_four]
    groups = lax.axis_size("group")
    locals_ = lax.axis_size("local")
    here = lax.axis_index("local")
    batch, tables = q_local.shape
    q_rows, _, width = q_tables.shape
    r_rows = r_tables.shape[0]
    share = -(-tables // locals_)
    padded = share * locals_
    extra = padded - tables

    q_major = jnp.transpose(jnp.pad(q_tables, ((0, 0), (0, extra), (0, 0))), (1, 0, 2))
    q_mine = lax.dynamic_slice_in_dim(q_major, here * share, share, 0)
    q_all = lax.all_gather(q_mine.astype(BF16), "group", axis=0, tiled=False)
    r_major = jnp.transpose(jnp.pad(r_tables, ((0, 0), (0, extra), (0, 0))), (1, 0, 2))
    q_index = (owner[:, :, 0] * q_rows + q_local).astype(F32)
    indices = jnp.stack([q_index, r_index.astype(F32)], axis=0)
    indices = jnp.transpose(jnp.pad(indices, ((0, 6), (0, 0), (0, extra))), (2, 0, 1))
    pack = jnp.concatenate([r_major, indices], axis=1)
    pack = pack.reshape(locals_, share, r_rows + 8, width)
    pack = lax.all_to_all(pack, "local", split_axis=0, concat_axis=0, tiled=True)

    def spec(lead, *tail):
        return pl.BlockSpec((lead, 1) + tail, lambda t: (0, t) + (0,) * len(tail))

    def flat(*tail):
        return pl.BlockSpec((1,) + tail, lambda t: (t,) + (0,) * len(tail))

    many = locals_ * batch
    work = 2 * share * many * width * (groups * q_rows + 6 * locals_ * r_rows)
    cost = pl.CostEstimate(flops=work, bytes_accessed=8 << 20, transcendentals=0)
    embeds, q_val, r_val = pl.pallas_call(
        lookup_kernel,
        grid=(share,),
        in_specs=[spec(groups, q_rows, width), spec(locals_, r_rows + 8, width)],
        out_specs=[spec(locals_, width, batch), flat(width, many), flat(width, many)],
        out_shape=[
            jax.ShapeDtypeStruct((locals_, share, width, batch), BF16),
            jax.ShapeDtypeStruct((share, width, many), BF16),
            jax.ShapeDtypeStruct((share, width, many), F32),
        ],
        cost_estimate=cost,
        name="lookup",
    )(q_all, pack)
    embeds = lax.all_to_all(embeds, "local", split_axis=0, concat_axis=0, tiled=True)
    embeds = embeds.reshape(padded, width, batch)

    dense_t = dense_vec.T
    steps = 4 * (-(-tables // 4))
    slots = max(steps, tables + 1)
    pairs = tables * (tables + 1) // 2
    row_slots = -(-(tables * (tables - 1) // 2 + steps) // 8) * 8
    vec_scratch = pltpu.VMEM((slots, width, batch), F32)
    pair_cost = pl.CostEstimate(
        flops=64 * pairs * width * batch, bytes_accessed=2 << 20, transcendentals=0
    )
    features_t = pl.pallas_call(
        functools.partial(gram_kernel, tables),
        in_specs=whole(2),
        out_specs=whole(1)[0],
        out_shape=jax.ShapeDtypeStruct((width + pairs, batch), BF16),
        scratch_shapes=[vec_scratch, pltpu.VMEM((row_slots, batch), F32)],
        cost_estimate=pair_cost,
        name="gram",
    )(dense_t, embeds)

    inputs = [None]
    pres = []
    current = None
    for k in range(4):
        if k == 0:
            pre = contract_rows(features_t, weights[0]) + biases[0]
        else:
            pre = jnp.dot(current, weights[k], preferred_element_type=F32) + biases[k]
        pres.append(pre)
        if k < 3:
            current = jax.nn.silu(pre).astype(BF16)
            inputs.append(current)
    grad_low = cotangent
    grad_full = cotangent.astype(F32)
    w_grads, b_grads = [None] * 4, [None] * 4
    for k in (3, 2, 1, 0):
        b_grads[k] = jnp.sum(grad_full, axis=0)
        if k:
            w_grads[k] = contract_rows(inputs[k], grad_low)
            back = lax.dot_general(
                grad_low, weights[k], (((1,), (1,)), ((), ())), preferred_element_type=F32
            )
            grad_full = back * silu_slope(pres[k - 1])
            grad_low = grad_full.astype(BF16)
        else:
            w_grads[0] = jnp.dot(features_t, grad_low, preferred_element_type=F32)
    d_features_t = lax.dot_general(
        w_one, grad_low, (((1,), (1,)), ((), ())), preferred_element_type=F32
    )

    d_embeds = pl.pallas_call(
        functools.partial(pair_kernel, tables),
        in_specs=whole(3),
        out_specs=whole(1)[0],
        out_shape=jax.ShapeDtypeStruct((padded, width, batch), BF16),
        scratch_shapes=[vec_scratch],
        cost_estimate=pair_cost,
        name="pair_back",
    )(d_features_t, dense_t, embeds)
    d_embeds = lax.all_to_all(
        d_embeds.reshape(locals_, share, width, batch),
        "local",
        split_axis=0,
        concat_axis=0,
        tiled=True,
    )
    q_part, r_part = pl.pallas_call(
        table_grad_kernel,
        grid=(share,),
        in_specs=[
            spec(locals_, width, batch),
            spec(locals_, r_rows + 8, width),
            flat(width, many),
            flat(width, many),
        ],
        out_specs=[spec(groups, q_rows, width), spec(locals_, r_rows, width)],
        out_shape=[
            jax.ShapeDtypeStruct((groups, share, q_rows, width), BF16),
            jax.ShapeDtypeStruct((locals_, share, r_rows, width), F32),
        ],
        cost_estimate=cost,
        name="table_grad",
    )(d_embeds, pack, q_val, r_val)

    q_piece = lax.psum_scatter(q_part, "group", scatter_dimension=0, tiled=False).astype(F32)
    q_mine_new = lax.all_gather(q_mine - table_rate * q_piece, "local", axis=0, tiled=False)
    q_new = jnp.transpose(q_mine_new.reshape(padded, q_rows, width)[:tables], (1, 0, 2))

    bias_sizes = [b.shape[0] for b in biases]
    bias_total = sum(bias_sizes)
    bias_rows = -(-bias_total // (8 * width)) * 8
    b_flat = jnp.concatenate(b_grads + [jnp.zeros((bias_rows * width - bias_total,), F32)])
    b_block = jnp.broadcast_to(
        b_flat.reshape(1, bias_rows, width), (locals_, bias_rows, width)
    )
    mixed = jnp.concatenate([r_part.reshape(locals_, share * r_rows, width), b_block], axis=1)
    mixed = lax.all_to_all(mixed, "local", split_axis=0, concat_axis=0, tiled=True)
    r_lines = mixed[:, : share * r_rows, :].reshape(padded * r_rows, width)
    b_lines = jnp.sum(mixed[:, share * r_rows :, :], axis=0)
    summed = lax.psum(jnp.concatenate([r_lines, b_lines], axis=0), "group")
    r_grad = summed[: tables * r_rows].reshape(tables, r_rows, width)
    r_new = r_tables - table_rate * jnp.transpose(r_grad, (1, 0, 2))
    b_sum = summed[padded * r_rows :].reshape(-1)

    w_sums = lax.psum([g.astype(BF16) for g in w_grads], ("group", "local"))
    updated = []
    start = 0
    for weight, bias, w_sum, size in zip(weights, biases, w_sums, bias_sizes):
        updated.append(weight.astype(F32) - dense_rate * w_sum.astype(F32))
        updated.append(bias - dense_rate * b_sum[start : start + size])
        start += size
    return (q_new, r_new) + tuple(updated)


def solution(mesh):
    rows = P(("group", "local"), None)
    return jax.shard_map(
        body,
        mesh=mesh,
        in_specs=(
            rows,
            P("group", None, None),
            P("local", None, None),
            P(("group", "local"), None, None),
            rows,
            rows,
            P(),
            P(),
            P(),
            P(),
            P(),
            P(),
            P(),
            P(),
            rows,
        ),
        out_specs=(P("group", None, None), P("local", None, None)) + (P(),) * 8,
        check_vma=False,
    )
```

time: 591 us -> 459 us (0.78)
  local copies, waits for them, and re-layouts: 130 us -> 10.8 us
  other arithmetic: 64.9 us -> 18.5 us
  Pallas kernels: 0 us -> 29.9 us
  waiting for transfers between devices: 290 us -> 317 us
  matrix products: 34 us -> 12.3 us
  starting transfers between devices: 15.7 us -> 3.86 us
  blocking collectives: 40.8 us -> 51.7 us
    gather x5 -> x0, local copies, waits for them, and re-layouts: 75.7 us -> none  [the longest x1 34.5 us: body(): outgoing = keys_padded[source].reshape(groups, capacity)]
    all_to_all x3 -> x1, waiting for transfers between devices: 81.4 us -> 12.2 us  [body(): lax.all_to_all(embeds, 'local', split_axis=0, concat_axis=0, tiled=True)]
    all_to_all x0 -> x3, blocking collectives: none -> 51.7 us  [the longest x1 18.4 us: body(): lax.all_to_all(pack, 'local', split_axis=0, concat_axis=0, tiled=True)]
    scatter-add x1 -> x0, other arithmetic: 45.6 us -> none  [body(): jax.ops.segment_sum(returned, served_flat, num_segments=segment_count)]
    psum x1 -> x0, blocking collectives: 40.8 us -> none  [body(): lax.psum((grads[0][0], grads[0][1], grads[1][0], grads[1][1], grads[2][0]...]
    all_gather x2, waiting for transfers between devices: 7.19 us -> 47.5 us  [the longest x1 32.1 us: body(): q_all = lax.all_gather(q_mine.astype(BF16), 'group', axis=0, tiled=False)]
    reduce_scatter x1, waiting for transfers between devices: 8.32 us -> 40.3 us  [body(): lax.psum_scatter(q_part, 'group', scatter_dimension=0, tiled=False)]
    scatter x2 -> x0, local copies, waits for them, and re-layouts: 31.8 us -> none  [the longest x1 19 us: pair_back(): spread = jnp.zeros((vectors_all.shape[0], vectors, vectors), jnp.float32)...]
  transfers between devices with their start and end apart: 7 -> 6, of which waited for: 6 -> 6; matrix products, arithmetic and copies ran while one was open for 18% -> 6% of each run, Pallas kernels for 0% -> 0%
where the time goes in v1:
time: 459 us; the launch traced here: 458 us
  waiting for transfers between devices  317 us (69%)
  blocking collectives  51.7 us (11%)
  Pallas kernels  29.9 us (7%)
  other arithmetic  18.5 us (4%)
  between operations  14.1 us (3%)
  matrix products  12.3 us (3%)
  local copies, waits for them, and re-layouts  10.8 us (2%)
    psum x1, waiting for transfers between devices, body(): w_sums = lax.psum([g.astype(BF16) for g in w_grads], ('group', 'local'))  148 us
    psum x1, waiting for transfers between devices, body(): summed = lax.psum(jnp.concatenate([r_lines, b_lines], axis=0), 'group')  68.8 us
    reduce_scatter x1, waiting for transfers between devices, body(): lax.psum_scatter(q_part, 'group', scatter_dimension=0, tiled=False)  40.3 us
    all_gather x1, waiting for transfers between devices, body(): q_all = lax.all_gather(q_mine.astype(BF16), 'group', axis=0, tiled=False)  32.1 us
    all_to_all x1, blocking collectives, body(): lax.all_to_all(pack, 'local', split_axis=0, concat_axis=0, tiled=True)  18.4 us
    all_to_all x1, blocking collectives, body(): lax.all_to_all(d_embeds.reshape(locals_, share, width, batch), 'local', s...  17.3 us
    all_to_all x1, blocking collectives, body(): lax.all_to_all(mixed, 'local', split_axis=0, concat_axis=0, tiled=True)  16 us
    all_gather x1, waiting for transfers between devices, body(): lax.all_gather(q_mine - table_rate * q_piece, 'local', axis=0, tiled=False)  15.4 us
  transfers between devices with their start and end apart: 6, of which 6 were waited for; matrix products, arithmetic and copies ran while one was open for 6% of the time, Pallas kernels for 0%

profile of v1, /device:TPU:0, one launch (start us, length us, event | category | flops | bytes accessed | tf_op | source)
XLA Modules:
  0.0 458.4 jit_solution(2653715238649833769)
XLA Ops:
  7.3 1.8 fusion.1
  9.4 18.4 %all_to_all.20.pack_ref = f32[4,7,72,128]{3,2,1,0:T(8,128)} all-to-all(f32[4,7,72,128]{3,2,1,0:T(8,128)S(1)} %bitcast.70), channel_id=1, replica_groups=mesh['group'=8,'local'=4] {'local'}, dimensions={0} | all-to-all | bytes 2064384 | tf_op jit(solution)/shard_map/all_to_all | solution.py:173
  27.8 32.1 %all-gather.5.cloned.1.call-done = bf16[56,128,128]{2,1,0:T(8,128)(2,1)} async-done(((bf16[7,128,128]{2,1,0:T(8,128)(2,1)}), bf16[56,128,128]{2,1,0:T(8,128)(2,1)}) %all-gather.5.cloned.1.call-update) | async-done | bytes 1835024 | tf_op jit(solution)/shard_map/all_gather | solution.py:166
  59.9 8.6 %lookup.1 = (bf16[4,7,128,128]{3,2,1,0:T(8,128)(2,1)}, bf16[7,128,512]{2,1,0:T(8,128)(2,1)}, f32[7,128,512]{2,1,0:T(8,128)}) custom-call(bf16[8,7,128,128]{3,2,1,0:T(8,128)(2,1)} %bitcast.80, f32[4,7,72,128]{3,2,1,0:T(8,128)} %all_to_all.20.pack_ref), custom_call_target="tpu_custom_call" | custom-call | flops 2348810240 | bytes 8388608 | tf_op jit(solution)/shard_map/lookup/pallas_call | solution.py:184
  68.6 3.6 all-to-all-start.1
  73.0 12.2 %all-to-all-done.1 = bf16[4,7,128,128]{3,2,1,0:T(8,128)(2,1)S(1)} async-done(((bf16[4,7,128,128]{3,2,1,0:T(8,128)(2,1)}), bf16[4,7,128,128]{3,2,1,0:T(8,128)(2,1)S(1)}, u32[]{:S(2)}, u32[]{:S(2)}) %all-to-all-start.1) | async-done | bytes 917536 | tf_op jit(solution)/shard_map/all_to_all | solution.py:197
  86.1 5.7 %gram.1 = bf16[479,128]{1,0:T(8,128)(2,1)} custom-call(bf16[128,128]{1,0:T(8,128)(2,1)} %bitcast.77, bf16[28,128,128]{2,1,0:T(8,128)(2,1)} %bitcast.72), custom_call_target="tpu_custom_call" | custom-call | flops 368050176 | bytes 2097152 | tf_op jit(solution)/shard_map/gram/pallas_call | solution.py:209
  91.8 1.2 convolution_add_fusion
  93.1 2.1 convolution_add_fusion.1
  97.1 1.1 copy-done.4
  99.1 1.1 convolution_bitcast_fusion.d_ref
  100.2 6.3 %pair_back.1 = bf16[28,128,128]{2,1,0:T(8,128)(2,1)} custom-call(f32[479,128]{1,0:T(8,128)} %convolution_bitcast_fusion.d_ref, bf16[128,128]{1,0:T(8,128)(2,1)} %bitcast.78, bf16[28,128,128]{2,1,0:T(8,128)(2,1)} %bitcast.73), custom_call_target="tpu_custom_call" | custom-call | flops 368050176 | bytes 2097152 | tf_op jit(solution)/shard_map/pair_back/pallas_call | solution.py:249
  106.6 17.3 %all_to_all.21.d_ref = bf16[4,7,128,128]{3,2,1,0:T(8,128)(2,1)} all-to-all(bf16[4,7,128,128]{3,2,1,0:T(8,128)(2,1)} %bitcast.74), channel_id=1, replica_groups=mesh['group'=8,'local'=4] {'local'}, dimensions={0} | all-to-all | bytes 1835008 | tf_op jit(solution)/shard_map/all_to_all | solution.py:258
  123.9 9.3 %table_grad.1 = (bf16[8,7,128,128]{3,2,1,0:T(8,128)(2,1)}, f32[4,7,64,128]{3,2,1,0:T(8,128)}) custom-call(bf16[4,7,128,128]{3,2,1,0:T(8,128)(2,1)} %all_to_all.21.d_ref, f32[4,7,72,128]{3,2,1,0:T(8,128)} %all_to_all.20.pack_ref, bf16[7,128,512]{2,1,0:T(8,128)(2,1)} %get-tuple-element.16.q_ref, f32[7,128,512]{2,1,0:T(8,128)} %get-tuple-element.17.r_ref), custom_call_target="tpu_custom_call" | custom-call | flops 2348810240 | bytes 8388608 | tf_op jit(solution)/shard_map/table_grad/pallas_call | solution.py:265
  134.3 1.3 convolution_convert_fusion.2
  135.6 1.5 convolution_convert_fusion.1
  137.1 2.1 convolution_convert_fusion
  140.4 16.0 %all_to_all.22 = f32[4,472,128]{2,1,0:T(8,128)S(1)} all-to-all(f32[4,472,128]{2,1,0:T(8,128)S(1)} %pad_maximum_fusion.1), channel_id=1, replica_groups=mesh['group'=8,'local'=4] {'local'}, dimensions={0} | all-to-all | bytes 1933312 | tf_op jit(solution)/shard_map/all_to_all | solution.py:295
  157.5 40.3 %reduce-scatter.2.cloned.1.call-done = bf16[1,7,128,128]{3,2,1,0:T(8,128)(2,1)} async-done(((bf16[8,7,128,128]{3,2,1,0:T(8,128)(2,1)}), bf16[1,7,128,128]{3,2,1,0:T(8,128)(2,1)}) %reduce-scatter.2.cloned.1.call-update) | async-done | bytes 229392 | tf_op jit(solution)/shard_map/reduce_scatter | solution.py:283
  197.8 1.8 bitcast_subtract_fusion
  199.7 148.3 %all-reduce.9.cloned.1.call-done = (bf16[479,1024]{1,0:T(8,128)(2,1)}, bf16[1024,1024]{1,0:T(8,128)(2,1)}, bf16[1024,512]{1,0:T(8,128)(2,1)}, bf16[512,256]{1,0:T(8,128)(2,1)}) async-done(((bf16[479,1024]{1,0:T(8,128)(2,1)}, bf16[1024,1024]{1,0:T(8,128)(2,1)}, bf16[1024,512]{1,0:T(8,128)(2,1)}, bf16[512,256]{1,0:T(8,128)(2,1)}), (bf16[479,1024]{1,0:T(8,128)(2,1)}, bf16[1024,1024]{1,0:T(8,128)(2,1)}, ...) | async-done | bytes 4388880 | tf_op jit(solution)/shard_map/psum | solution.py:303
  348.0 1.9 multiply_subtract_fusion.3
  349.9 3.0 multiply_subtract_fusion.2
  352.9 1.6 multiply_subtract_fusion.1
  355.9 2.9 multiply_subtract_fusion
  358.8 68.8 %all-reduce.7.cloned.1.call-done = f32[1816,128]{1,0:T(8,128)} async-done(((f32[1816,128]{1,0:T(8,128)}), f32[1816,128]{1,0:T(8,128)}) %all-reduce.7.cloned.1.call-update) | async-done | bytes 929808 | tf_op jit(solution)/shard_map/psum | solution.py:298
  427.6 1.2 slice_multiply_fusion
  429.9 1.2 fusion.19
  431.1 1.3 fusion.17
  432.4 1.3 fusion.13
  433.7 15.4 %all-gather.7.cloned.1.call-done = f32[28,128,128]{2,1,0:T(8,128)} async-done(((f32[7,128,128]{2,1,0:T(8,128)}), f32[28,128,128]{2,1,0:T(8,128)}) %all-gather.7.cloned.1.call-update) | async-done | bytes 1835024 | tf_op jit(solution)/shard_map/all_gather | solution.py:284
  449.1 2.8 slice_bitcast_fusion
  (80 shorter events, 10.6 us)
Async XLA Ops:
  7.2 1.9 copy-start.16
  7.2 1.9 copy-start.18
  7.2 1.9 copy-start.17
  7.2 2.0 copy-start.3
  7.2 52.7 %all-gather.5.cloned.1.call-start = ((), (), s32[]{:S(2)}) async-start(), calls=%async_computation.7 | async-start | bytes 2064384 | tf_op jit(solution)/shard_map/all_gather | solution.py:166
  59.9 12.3 %copy-start.14 = (bf16[128,128]{1,0:T(8,128)(2,1)S(1)}, bf16[128,128]{1,0:T(8,128)(2,1)}, u32[]{:S(2)}) copy-start(bf16[128,128]{1,0:T(8,128)(2,1)} %param.15) | copy-start | bytes 98308
  68.5 23.2 %copy-start = (bf16[479,1024]{1,0:T(8,128)(2,1)S(1)}, bf16[479,1024]{1,0:T(8,128)(2,1)}, u32[]{:S(2)}) copy-start(bf16[479,1024]{1,0:T(8,128)(2,1)} %param.21) | copy-start | bytes 2942980
  68.5 23.2 %copy-start.15 = (f32[1024]{0:T(1024)S(1)}, f32[1024]{0:T(1024)}, u32[]{:S(2)}) copy-start(f32[1024]{0:T(1024)} %param.22) | copy-start | bytes 12292
  68.6 24.5 %copy-start.19 = (f32[1024]{0:T(1024)S(1)}, f32[1024]{0:T(1024)}, u32[]{:S(2)}) copy-start(f32[1024]{0:T(1024)} %param.24) | copy-start | bytes 12292
  68.6 16.7 %all-to-all-start.1 = ((bf16[4,7,128,128]{3,2,1,0:T(8,128)(2,1)}), bf16[4,7,128,128]{3,2,1,0:T(8,128)(2,1)S(1)}, u32[]{:S(2)}, u32[]{:S(2)}) async-start(bf16[4,7,128,128]{3,2,1,0:T(8,128)(2,1)} %get-tuple-element.15), calls=%async_computation.1 | async-start | bytes 1835008 | tf_op jit(solution)/shard_map/all_to_all | solution.py:197
  72.2 125.6 %reduce-scatter.2.cloned.1.call-start = ((), (), s32[]{:S(2)}) async-start(), calls=%async_computation.5 | async-start | bytes 2064384 | tf_op jit(solution)/shard_map/reduce_scatter | solution.py:283
  85.2 0.9 copy-start.2
  93.0 2.2 copy-start.7
  93.1 2.2 copy-start.20
  95.2 1.4 copy-start.22
  95.2 1.1 copy-start.12
  95.3 1.1 copy-start.13
  96.6 1.6 copy-start.4
  133.2 1.1 copy-start.11
  133.2 214.8 %all-reduce.9.cloned.1.call-start = ((), (), s32[]{:S(2)}) async-start(), calls=%async_computation.9 | async-start | bytes 8781824 | tf_op jit(solution)/shard_map/psum | solution.py:303
  133.3 2.4 copy-start.23
  139.2 1.2 copy-start.10
  139.2 288.4 %all-reduce.7.cloned.1.call-start = ((), (), s32[]{:S(2)}) async-start(), calls=%async_computation.6 | async-start | bytes 1859584 | tf_op jit(solution)/shard_map/psum | solution.py:298
  156.4 41.5 %copy-start.1 = (f32[128,26,128]{2,0,1:T(8,128)S(1)}, f32[128,26,128]{2,0,1:T(8,128)}, u32[]{:S(2)}) copy-start(f32[128,26,128]{2,0,1:T(8,128)} %param.16) | copy-start | bytes 5111812
  157.5 291.6 %all-gather.7.cloned.1.call-start = ((), (), s32[]{:S(2)}) async-start(), calls=%async_computation.8 | async-start | bytes 2293760 | tf_op jit(solution)/shard_map/all_gather | solution.py:284
  349.9 3.0 copy-start.8
  349.9 3.0 copy-start.9
  352.9 2.3 copy-start.5
  352.9 3.0 copy-start.6
  358.8 71.1 %copy-start.21 = (f32[256]{0:T(256)S(1)}, f32[256]{0:T(256)}, u32[]{:S(2)}) copy-start(f32[256]{0:T(256)} %param.28) | copy-start | bytes 3076
Sparse Core Ops, SparseCore 0:
  10.8 49.0 all-gather.4
  133.3 64.4 reduce-scatter.1
  204.6 143.3 all-reduce.8
  351.3 76.2 all-reduce.6
  429.0 20.0 all-gather.6
